TPU v7x, 256 devices: a whole 4x4x8 slice. The times are simulated.
256 devices in a mesh: space: 8 (over y_hi, x), vel: 32 (over z, y_lo, core).
Axes of the slice: x: 4, y: 4 (y_hi: 2, y_lo: 2; y = y_hi * 2 + y_lo), z: 8, core: 2. Of those that a mesh axis runs over, the one named last changes fastest.
Arguments:
- distribution: float32 [8, 16, 16, 32768], P('space', None, None, 'vel'), may hold values from 0.003 to 450, as said below
- inflow: float32 [2, 16, 16, 32768], P(None, None, None, 'vel'), may hold values from 0.3 to 3
- wall_temp: float32 [2, 16, 16], replicated, may hold values from 0.5 to 4
- face_type: int32 [2, 16, 16], replicated, may hold values from 0 to 2
Outputs:
- updated: float32 [8, 16, 16, 32768], P('space', None, None, 'vel')
- fields: float32 [8, 8, 16, 16], P(None, 'space')
Inputs may be any that keep to these rules, and one draw needn't show every extreme that they name: `distribution`: every entry is positive.
All inputs are finite; a program needn't handle non-finite values.
Results may differ from a plain program's by a relative error of at most 0.0003.
Values sent between devices are 32-bit elements; how exact they have to be, the bound alone decides.
No kernel may reach another device: no remote copies, remote signals or barrier semaphores. Data moves between devices by JAX's collectives and lax.ppermute only.
A program may use at most 64 MiB of HBM per device.

v0:
```python
import jax
import jax.numpy as jnp
from jax import lax
from jax.sharding import PartitionSpec as P

NVX = 32
NVY = 32
NVZ = 32
OUTER = 2
INNER = 3
box_volume = 512.0
speed_top = 4.0
courant = 0.08
impact_rate_field = 0.8
shakhov_factor = 1.0 / 3.0


def padded_2(cells, sides, width):
    for axis, dim in sides:
        count = lax.axis_size(axis)
        ends = count - 1
        head = lax.slice_in_dim(cells, 0, width, axis=dim)
        tail = lax.slice_in_dim(cells, cells.shape[dim] - width, cells.shape[dim], axis=dim)
        cells = jnp.concatenate(
            [
                lax.ppermute(tail, axis, [(i, (i + 1) % count) for i in range(ends)]),
                cells,
                lax.ppermute(head, axis, [((i + 1) % count, i) for i in range(ends)]),
            ],
            axis=dim,
        )
    return cells


def velocity_table(count_x, count_y, count_z, shards):
    velocity_total = count_x * count_y * count_z
    velocity_index = jnp.arange(velocity_total, dtype=jnp.int32)
    per_shard = velocity_total // shards
    halves = per_shard // 2
    owner_shard = velocity_index // per_shard
    within = velocity_index % per_shard
    upper_half = within // halves
    ranked = owner_shard * halves + within % halves
    layer_size = count_y * count_z
    level_x = ranked // layer_size
    remain = ranked % layer_size
    across_y = remain // count_z
    across_z = remain % count_z
    sign_x = 2.0 * upper_half.astype(jnp.float32) - 1.0
    speed_x = sign_x * (level_x.astype(jnp.float32) + 0.5) * (2.0 * speed_top / count_x)
    speed_y = (across_y.astype(jnp.float32) + 0.5) * (2.0 * speed_top / count_y) - speed_top
    speed_z = (across_z.astype(jnp.float32) + 0.5) * (2.0 * speed_top / count_z) - speed_top
    return (speed_x, speed_y, speed_z)


def wall_shape(wall_temp, speed_sq):
    temp_cell = wall_temp[..., None]
    return box_volume * jnp.exp(-speed_sq / (2.0 * temp_cell)) / (2.0 * jnp.pi * temp_cell) ** 1.5


def boundary_planes(edge_planes, leaving, entering, wall_profile, inflow, face_type):
    wall_planes = (leaving / entering)[..., None] * wall_profile
    face_kind = face_type[..., None]
    return jnp.where(face_kind == 0, wall_planes, jnp.where(face_kind == 1, inflow, edge_planes))


def transport(current, west_plane, east_plane, speed_x, speed_y, speed_z):
    west_cells = jnp.concatenate([west_plane[None], current[:-1]], 0)
    east_cells = jnp.concatenate([current[1:], east_plane[None]], 0)
    flux_sum = jnp.maximum(speed_x, 0.0) * (current - west_cells) + jnp.minimum(speed_x, 0.0) * (
        east_cells - current
    )
    flux_sum = (
        flux_sum
        + jnp.maximum(speed_y, 0.0) * (current - jnp.roll(current, 1, 1))
        + jnp.minimum(speed_y, 0.0) * (jnp.roll(current, -1, 1) - current)
    )
    flux_sum = (
        flux_sum
        + jnp.maximum(speed_z, 0.0) * (current - jnp.roll(current, 1, 2))
        + jnp.minimum(speed_z, 0.0) * (jnp.roll(current, -1, 2) - current)
    )
    return current - courant * flux_sum


def macro_fields(
    particle_concentration,
    mean_motion_first_axis,
    mean_motion_second_axis,
    mean_motion_third_axis,
    maxwellian_width,
    energy_current_first,
    energy_current_second,
    energy_current_third,
):
    kinetic_warmth = maxwellian_width / (3.0 * particle_concentration)
    decay_rate_toward_target = (
        impact_rate_field * particle_concentration * jnp.exp(0.19 * jnp.log(kinetic_warmth))
    )
    return jnp.stack(
        [
            particle_concentration,
            mean_motion_first_axis,
            mean_motion_second_axis,
            mean_motion_third_axis,
            kinetic_warmth,
            energy_current_first,
            energy_current_second,
            energy_current_third,
            decay_rate_toward_target,
        ]
    )


def shakhov(params, speed_x, speed_y, speed_z):
    particle_concentration = params[0][..., None]
    peculiar_x = speed_x - params[1][..., None]
    peculiar_y = speed_y - params[2][..., None]
    peculiar_z = speed_z - params[3][..., None]
    temp_cell = params[4][..., None]
    speed_sq = peculiar_x * peculiar_x + peculiar_y * peculiar_y + peculiar_z * peculiar_z
    maxwell = (
        particle_concentration
        * box_volume
        * jnp.exp(-speed_sq / (2.0 * temp_cell))
        / (2.0 * jnp.pi * temp_cell) ** 1.5
    )
    heat_term = (
        params[5][..., None] * peculiar_x
        + params[6][..., None] * peculiar_y
        + params[7][..., None] * peculiar_z
    ) / (5.0 * particle_concentration * temp_cell * temp_cell)
    return maxwell * (1.0 + shakhov_factor * heat_term * (speed_sq / temp_cell - 5.0))


def relaxation(read, params, speed_x, speed_y, speed_z):
    decay_rate_toward_target = params[8][..., None]
    return (read + decay_rate_toward_target * shakhov(params, speed_x, speed_y, speed_z)) / (
        1.0 + decay_rate_toward_target
    )


def moment_fields(current, moment_table, speed_x, speed_y, speed_z, velocity_total):
    cell_count = current.shape[0] * current.shape[1] * current.shape[2]
    flattened = current.reshape(cell_count, current.shape[3])
    partial_value = jnp.einsum(
        "cv,vk->kc", flattened, moment_table[:, :4], precision=lax.Precision.HIGHEST
    )
    first_sum = lax.psum(partial_value, "vel") / velocity_total
    particle_concentration = first_sum[0]
    mean_motion_first_axis = first_sum[1] / particle_concentration
    mean_motion_second_axis = first_sum[2] / particle_concentration
    mean_motion_third_axis = first_sum[3] / particle_concentration
    peculiar_x = speed_x[None, :] - mean_motion_first_axis[:, None]
    peculiar_y = speed_y[None, :] - mean_motion_second_axis[:, None]
    peculiar_z = speed_z[None, :] - mean_motion_third_axis[:, None]
    speed_sq = peculiar_x * peculiar_x + peculiar_y * peculiar_y + peculiar_z * peculiar_z
    weighted = flattened * speed_sq
    second = jnp.stack(
        [
            jnp.sum(weighted, 1),
            0.5 * jnp.sum(weighted * peculiar_x, 1),
            0.5 * jnp.sum(weighted * peculiar_y, 1),
            0.5 * jnp.sum(weighted * peculiar_z, 1),
        ]
    )
    second = lax.psum(second, "vel") / velocity_total
    params = macro_fields(
        particle_concentration,
        mean_motion_first_axis,
        mean_motion_second_axis,
        mean_motion_third_axis,
        second[0],
        second[1],
        second[2],
        second[3],
    )
    return params.reshape((9,) + current.shape[:3])


def body(distribution, inflow, wall_temp, face_type):
    velocity_total = NVX * NVY * NVZ
    local_count = distribution.shape[3]
    full_x, full_y, full_z = velocity_table(NVX, NVY, NVZ, lax.axis_size("vel"))
    offset = lax.axis_index("vel") * local_count
    speed_x = lax.dynamic_slice_in_dim(full_x, offset, local_count)
    speed_y = lax.dynamic_slice_in_dim(full_y, offset, local_count)
    speed_z = lax.dynamic_slice_in_dim(full_z, offset, local_count)
    speed_sq = speed_x * speed_x + speed_y * speed_y + speed_z * speed_z
    moment_table = jnp.stack(
        [
            jnp.ones_like(speed_x),
            speed_x,
            speed_y,
            speed_z,
            speed_x * speed_x,
            speed_y * speed_y,
            speed_z * speed_z,
            speed_x * speed_y,
            speed_x * speed_z,
            speed_y * speed_z,
            0.5 * speed_x * speed_sq,
            0.5 * speed_y * speed_sq,
            0.5 * speed_z * speed_sq,
        ],
        1,
    )
    lowest_slab = lax.axis_index("space") == 0
    highest_slab = lax.axis_index("space") == lax.axis_size("space") - 1
    wall_profile = wall_shape(wall_temp, speed_sq)
    outward = jnp.stack([-speed_x, speed_x])[:, None, None, :]
    entering_part = jnp.sum(wall_profile * jnp.maximum(-outward, 0.0), -1)
    current = distribution
    params = None
    for outer_turn in range(OUTER):
        edge_planes = jnp.stack([current[0], current[-1]])
        leaving_part = jnp.sum(edge_planes * jnp.maximum(outward, 0.0), -1)
        leaving, entering = lax.psum((leaving_part, entering_part), "vel")
        ghost_planes = boundary_planes(
            edge_planes, leaving, entering, wall_profile, inflow, face_type
        )
        padded = padded_2(current, (("space", 0),), 1)
        west_plane = jnp.where(lowest_slab, ghost_planes[0], padded[0])
        east_plane = jnp.where(highest_slab, ghost_planes[1], padded[-1])
        read = transport(current, west_plane, east_plane, speed_x, speed_y, speed_z)
        current = read
        for inner_turn in range(INNER):
            params = moment_fields(current, moment_table, speed_x, speed_y, speed_z, velocity_total)
            current = relaxation(read, params, speed_x, speed_y, speed_z)
    return (current, params[:8])


def solution(mesh):
    in_specs = (P("space", None, None, "vel"), P(None, None, None, "vel"), P(), P())
    out_specs = (P("space", None, None, "vel"), P(None, "space", None, None))
    return jax.shard_map(body, mesh=mesh, in_specs=in_specs, out_specs=out_specs, check_vma=False)
```

profile of v0, /device:TPU:23, one launch (start us, length us, event | category | flops | bytes accessed | tf_op | source)
XLA Modules:
  0.0 943.6 jit_solution(8310820581644365251)
XLA Ops:
  0.6 1.4 collective-permute-start
  2.1 5.0 collective-permute-start.1
  7.1 0.8 negate_select_fusion
  7.8 0.8 negate_select_fusion.1
  8.6 0.7 negate_select_fusion.3
  9.3 0.7 negate_select_fusion.6
  10.0 0.7 broadcast_compare_fusion
  10.7 0.7 broadcast_compare_fusion.1
  11.4 0.6 fusion.186
  12.1 0.7 fusion.187
  12.8 0.7 sign_compare_fusion
  13.5 0.7 sign_compare_fusion.1
  14.1 2.3 constant_dynamic-update-slice_fusion.1
  16.5 1.2 fusion.249
  17.8 1.1 constant_dynamic-update-slice_fusion
  19.5 0.8 broadcast_maximum_fusion.2
  20.4 0.7 multiply_reduce_fusion
  21.0 1.8 multiply_reduce_fusion.1
  22.9 106.7 %all-reduce = (f32[2,16,16]{2,1,0:T(8,128)S(1)}, f32[2,16,16]{2,1,0:T(8,128)S(1)}) all-reduce(f32[2,16,16]{2,1,0:T(8,128)S(1)} %multiply_reduce_fusion.1, f32[2,16,16]{2,1,0:T(8,128)S(1)} %multiply_reduce_fusion), channel_id=1, replica_groups=mesh['space'=8,'vel'=32] {'vel'}, use_global_device_ids=true, to_apply=%region_1.2 | all-reduce | flops 1024 | bytes 8192 | tf_op jit(solution)/shard_map/psum | solution.py:218
  129.8 1.4 copy-done.1
  131.2 0.6 copy-done.2
  131.8 0.9 select_select_fusion
  132.7 0.9 copy-done.6
  133.7 2.4 fusion.163
  136.1 0.9 fusion.229
  137.0 56.8 %psum.110 = f32[4,256]{1,0:T(4,128)S(1)} all-reduce(f32[4,256]{1,0:T(4,128)S(1)} %fusion.229), channel_id=1, replica_groups=mesh['space'=8,'vel'=32] {'vel'}, use_global_device_ids=true, to_apply=%region_4.5 | all-reduce | flops 1024 | bytes 8192 | tf_op jit(solution)/shard_map/psum | solution.py:149
  194.1 0.9 fusion.235
  195.3 53.0 %psum.111 = f32[4,256]{1,0:T(4,128)S(1)} all-reduce(f32[4,256]{1,0:T(4,128)S(1)} %pad_maximum_fusion.3), channel_id=1, replica_groups=mesh['space'=8,'vel'=32] {'vel'}, use_global_device_ids=true, to_apply=%region_9.10 | all-reduce | flops 1024 | bytes 8192 | tf_op jit(solution)/shard_map/psum | solution.py:167
  249.0 1.3 fusion.28
  250.2 0.9 fusion.228
  251.2 53.0 %psum.112 = f32[4,256]{1,0:T(4,128)S(1)} all-reduce(f32[4,256]{1,0:T(4,128)S(1)} %fusion.228), channel_id=1, replica_groups=mesh['space'=8,'vel'=32] {'vel'}, use_global_device_ids=true, to_apply=%region_10.11 | all-reduce | flops 1024 | bytes 8192 | tf_op jit(solution)/shard_map/psum | solution.py:149
  304.4 2.1 fusion.234
  306.9 53.0 %psum.113 = f32[4,256]{1,0:T(4,128)S(1)} all-reduce(f32[4,256]{1,0:T(4,128)S(1)} %pad_maximum_fusion.4), channel_id=1, replica_groups=mesh['space'=8,'vel'=32] {'vel'}, use_global_device_ids=true, to_apply=%region_15.16 | all-reduce | flops 1024 | bytes 8192 | tf_op jit(solution)/shard_map/psum | solution.py:167
  360.5 1.3 fusion.51
  361.8 0.9 fusion.227
  362.7 53.2 %psum.114 = f32[4,256]{1,0:T(4,128)S(1)} all-reduce(f32[4,256]{1,0:T(4,128)S(1)} %fusion.227), channel_id=1, replica_groups=mesh['space'=8,'vel'=32] {'vel'}, use_global_device_ids=true, to_apply=%region_16.17 | all-reduce | flops 1024 | bytes 8192 | tf_op jit(solution)/shard_map/psum | solution.py:149
  416.2 2.1 fusion.233
  418.6 53.0 %psum.115 = f32[4,256]{1,0:T(4,128)S(1)} all-reduce(f32[4,256]{1,0:T(4,128)S(1)} %pad_maximum_fusion.5), channel_id=1, replica_groups=mesh['space'=8,'vel'=32] {'vel'}, use_global_device_ids=true, to_apply=%region_21.22 | all-reduce | flops 1024 | bytes 8192 | tf_op jit(solution)/shard_map/psum | solution.py:167
  472.2 1.3 fusion.74
  473.5 1.2 fusion.245
  474.7 1.3 collective-permute-start.2
  476.0 5.0 collective-permute-start.3
  481.3 113.0 %psum.116 = f32[2,16,16]{2,1,0:T(8,128)S(1)} all-reduce(f32[2,16,16]{2,1,0:T(8,128)S(1)} %fusion.4), channel_id=1, replica_groups=mesh['space'=8,'vel'=32] {'vel'}, use_global_device_ids=true, to_apply=%region_23.24 | all-reduce | flops 512 | bytes 4096 | tf_op jit(solution)/shard_map/psum | solution.py:218
  594.6 1.3 copy-done.3
  596.0 0.9 fusion.5
  597.1 5.7 fusion.152
  602.9 0.9 fusion.226
  603.8 56.8 %psum.117 = f32[4,256]{1,0:T(4,128)S(1)} all-reduce(f32[4,256]{1,0:T(4,128)S(1)} %fusion.226), channel_id=1, replica_groups=mesh['space'=8,'vel'=32] {'vel'}, use_global_device_ids=true, to_apply=%region_24.25 | all-reduce | flops 1024 | bytes 8192 | tf_op jit(solution)/shard_map/psum | solution.py:149
  660.8 0.9 fusion.232
  662.1 53.0 %psum.118 = f32[4,256]{1,0:T(4,128)S(1)} all-reduce(f32[4,256]{1,0:T(4,128)S(1)} %pad_maximum_fusion.6), channel_id=1, replica_groups=mesh['space'=8,'vel'=32] {'vel'}, use_global_device_ids=true, to_apply=%region_29.30 | all-reduce | flops 1024 | bytes 8192 | tf_op jit(solution)/shard_map/psum | solution.py:167
  715.7 1.3 fusion.97
  717.0 0.9 fusion.225
  717.9 53.0 %psum.119 = f32[4,256]{1,0:T(4,128)S(1)} all-reduce(f32[4,256]{1,0:T(4,128)S(1)} %fusion.225), channel_id=1, replica_groups=mesh['space'=8,'vel'=32] {'vel'}, use_global_device_ids=true, to_apply=%region_30.31 | all-reduce | flops 1024 | bytes 8192 | tf_op jit(solution)/shard_map/psum | solution.py:149
  771.2 2.1 fusion.231
  773.6 53.2 %psum.120 = f32[4,256]{1,0:T(4,128)S(1)} all-reduce(f32[4,256]{1,0:T(4,128)S(1)} %pad_maximum_fusion.7), channel_id=1, replica_groups=mesh['space'=8,'vel'=32] {'vel'}, use_global_device_ids=true, to_apply=%region_35.36 | all-reduce | flops 1024 | bytes 8192 | tf_op jit(solution)/shard_map/psum | solution.py:167
  827.5 1.3 fusion.120
  828.8 0.9 fusion.224
  829.7 53.0 %psum.121 = f32[4,256]{1,0:T(4,128)S(1)} all-reduce(f32[4,256]{1,0:T(4,128)S(1)} %fusion.224), channel_id=1, replica_groups=mesh['space'=8,'vel'=32] {'vel'}, use_global_device_ids=true, to_apply=%region_36.37 | all-reduce | flops 1024 | bytes 8192 | tf_op jit(solution)/shard_map/psum | solution.py:149
  883.2 0.7 fusion.237
  884.1 2.1 fusion.230
  886.5 53.0 %psum.122 = f32[4,256]{1,0:T(4,128)S(1)} all-reduce(f32[4,256]{1,0:T(4,128)S(1)} %pad_maximum_fusion.8), channel_id=1, replica_groups=mesh['space'=8,'vel'=32] {'vel'}, use_global_device_ids=true, to_apply=%region_41.42 | all-reduce | flops 1024 | bytes 8192 | tf_op jit(solution)/shard_map/psum | solution.py:167
  939.5 0.7 slice_reduce_fusion.2
  940.3 0.7 slice.445
  941.6 2.0 fusion.143
  (208 shorter events, 9.8 us)
Async XLA Ops:
  0.6 15.8 %copy-start = (f32[1,16,16,1024]{3,2,1,0:T(8,128)S(1)}, f32[1,16,16,1024]{3,2,1,0:T(8,128)}, u32[]{:S(2)}) copy-start(f32[1,16,16,1024]{3,2,1,0:T(8,128)} %param.4) | copy-start | bytes 3145732
  0.6 132.1 %collective-permute-start = (f32[1,16,16,1024]{3,2,1,0:T(8,128)}, f32[1,16,16,1024]{3,2,1,0:T(8,128)S(1)}, u32[]{:S(2)}, u32[]{:S(2)}) collective-permute-start(f32[1,16,16,1024]{3,2,1,0:T(8,128)} %param.4), channel_id=1, source_target_pairs={{0,32},{32,64},{64,96},{96,128},{128,160},{160,192},{192,224},{1,3... | collective-permute-start | bytes 3145736 | tf_op jit(solution)/shard_map/ppermute | solution.py:26
  2.1 130.7 %collective-permute-start.1 = (f32[1,16,16,1024]{3,2,1,0:T(8,128)}, f32[1,16,16,1024]{3,2,1,0:T(8,128)}, u32[]{:S(2)}, u32[]{:S(2)}) collective-permute-start(f32[1,16,16,1024]{3,2,1,0:T(8,128)} %param.4), channel_id=1, source_target_pairs={{32,0},{64,32},{96,64},{128,96},{160,128},{192,160},{224,192},{33,... | collective-permute-start | bytes 3145736 | tf_op jit(solution)/shard_map/ppermute | solution.py:28
  16.5 1.3 copy-start.25
  17.7 1.3 copy-start.26
  20.3 113.4 %copy-start.7 = (f32[1024]{0:T(1024)}, f32[1024]{0:T(1024)S(1)}, u32[]{:S(2)}) copy-start(f32[1024]{0:T(1024)S(1)} %get-tuple-element.130) | copy-start | bytes 12292
  20.3 113.4 %copy-start.9 = (f32[1024]{0:T(1024)}, f32[1024]{0:T(1024)S(1)}, u32[]{:S(2)}) copy-start(f32[1024]{0:T(1024)S(1)} %get-tuple-element.184) | copy-start | bytes 12292
  20.3 109.5 %copy-start.21 = (f32[1024]{0:T(1024)}, f32[1024]{0:T(1024)S(1)}, u32[]{:S(2)}) copy-start(f32[1024]{0:T(1024)S(1)} %get-tuple-element.180) | copy-start | bytes 12292
  20.3 113.4 %copy-start.11 = (f32[1024]{0:T(1024)}, f32[1024]{0:T(1024)S(1)}, u32[]{:S(2)}) copy-start(f32[1024]{0:T(1024)S(1)} %get-tuple-element.179) | copy-start | bytes 12292
  20.3 113.4 %copy-start.13 = (f32[1024]{0:T(1024)}, f32[1024]{0:T(1024)S(1)}, u32[]{:S(2)}) copy-start(f32[1024]{0:T(1024)S(1)} %get-tuple-element.181) | copy-start | bytes 12292
  20.4 113.3 %copy-start.15 = (f32[1024]{0:T(1024)}, f32[1024]{0:T(1024)S(1)}, u32[]{:S(2)}) copy-start(f32[1024]{0:T(1024)S(1)} %get-tuple-element.182) | copy-start | bytes 12292
  22.9 107.0 %copy-start.17 = (pred[2,16,16]{2,1,0:T(8,128)(4,1)S(1)}, pred[2,16,16]{2,1,0:T(8,128)(4,1)}, u32[]{:S(2)}) copy-start(pred[2,16,16]{2,1,0:T(8,128)(4,1)} %get-tuple-element.132) | copy-start | bytes 1540
  22.9 107.0 %copy-start.19 = (pred[2,16,16]{2,1,0:T(8,128)(4,1)S(1)}, pred[2,16,16]{2,1,0:T(8,128)(4,1)}, u32[]{:S(2)}) copy-start(pred[2,16,16]{2,1,0:T(8,128)(4,1)} %get-tuple-element.133) | copy-start | bytes 1540
  129.6 232.2 %copy-start.23 = (f32[4]{0:T(128)}, f32[4]{0:T(128)S(1)}, u32[]{:S(2)}) copy-start(f32[4]{0:T(128)S(1)} %pad.34.clone) | copy-start | bytes 52
  129.6 1.6 copy-start.1
  129.6 2.2 copy-start.2
  131.8 1.9 copy-start.4
  132.7 1.0 copy-start.6
  474.7 122.2 %collective-permute-start.2 = (f32[1,16,16,1024]{3,2,1,0:T(8,128)S(1)}, f32[1,16,16,1024]{3,2,1,0:T(8,128)}, u32[]{:S(2)}, u32[]{:S(2)}) collective-permute-start(f32[1,16,16,1024]{3,2,1,0:T(8,128)S(1)} %fusion.74), channel_id=1, source_target_pairs={{0,32},{32,64},{64,96},{96,128},{128,160},{160,192},{192,224},{1,3... | collective-permute-start | bytes 3145736 | tf_op jit(solution)/shard_map/ppermute | solution.py:26
  476.0 120.9 %collective-permute-start.3 = (f32[1,16,16,1024]{3,2,1,0:T(8,128)S(1)}, f32[1,16,16,1024]{3,2,1,0:T(8,128)}, u32[]{:S(2)}, u32[]{:S(2)}) collective-permute-start(f32[1,16,16,1024]{3,2,1,0:T(8,128)S(1)} %fusion.74), channel_id=1, source_target_pairs={{32,0},{64,32},{96,64},{128,96},{160,128},{192,160},{224,192},{33,... | collective-permute-start | bytes 3145736 | tf_op jit(solution)/shard_map/ppermute | solution.py:28
  594.3 1.6 copy-start.3
  594.3 1.6 copy-start.18
  594.3 1.6 copy-start.20
  594.3 1.6 copy-start.22
  595.9 1.2 copy-start.5
  595.9 1.2 copy-start.8
  595.9 1.2 copy-start.10
  595.9 1.2 copy-start.12
  595.9 1.2 copy-start.14
  596.0 1.2 copy-start.16
  597.1 5.7 copy-start.24
where the time goes:
time: 944 us
  blocking collectives  864 us (92%)
  other arithmetic  41.6 us (4%)
  local copies, waits for them, and re-layouts  18.9 us (2%)
  starting transfers between devices  12.7 us (1%)
    psum x6, blocking collectives, moment_fields(): first_sum = lax.psum(partial_value, 'vel') / velocity_total  326 us
    psum x6, blocking collectives, moment_fields(): second = lax.psum(second, 'vel') / velocity_total  318 us
    psum x2, blocking collectives, body(): leaving, entering = lax.psum((leaving_part, entering_part), 'vel')  220 us
  transfers between devices with their start and end apart: 4, of which 0 were waited for; matrix products, arithmetic and copies ran while one was open for 2% of the time, Pallas kernels for 0%

commit v1 on v0

--- a/solution.py
+++ b/solution.py
@@ -13,6 +13,11 @@
 courant = 0.08
 impact_rate_field = 0.8
 shakhov_factor = 1.0 / 3.0
+
+
+def add_all(block, axis):
+    parts = lax.all_gather(block, axis)
+    return jnp.sum(parts, axis=0)
 
 
 def padded_2(cells, sides, width):
@@ -146,7 +151,7 @@
     partial_value = jnp.einsum(
         "cv,vk->kc", flattened, moment_table[:, :4], precision=lax.Precision.HIGHEST
     )
-    first_sum = lax.psum(partial_value, "vel") / velocity_total
+    first_sum = add_all(partial_value, "vel") / velocity_total
     particle_concentration = first_sum[0]
     mean_motion_first_axis = first_sum[1] / particle_concentration
     mean_motion_second_axis = first_sum[2] / particle_concentration

time: 944 us -> 821 us (0.87)
  blocking collectives: 864 us -> 738 us
    psum x6 -> x0, blocking collectives: 326 us -> none  [moment_fields(): first_sum = lax.psum(partial_value, 'vel') / velocity_total]
    all_gather x0 -> x6, blocking collectives: none -> 203 us  [add_all(): parts = lax.all_gather(block, axis)]
where the time goes in v1:
time: 821 us; the launch traced here: 818 us
  blocking collectives  738 us (90%)
  other arithmetic  41.8 us (5%)
  local copies, waits for them, and re-layouts  18.9 us (2%)
  starting transfers between devices  12.7 us (2%)
    psum x6, blocking collectives, moment_fields(): second = lax.psum(second, 'vel') / velocity_total  315 us
    psum x2, blocking collectives, body(): leaving, entering = lax.psum((leaving_part, entering_part), 'vel')  220 us
    all_gather x6, blocking collectives, add_all(): parts = lax.all_gather(block, axis)  203 us
  transfers between devices with their start and end apart: 4, of which 0 were waited for; matrix products, arithmetic and copies ran while one was open for 2% of the time, Pallas kernels for 0%

profile of v1, /device:TPU:23, one launch (start us, length us, event | category | flops | bytes accessed | tf_op | source)
XLA Modules:
  0.0 818.2 jit_solution(700167760413803789)
XLA Ops:
  0.6 1.4 collective-permute-start
  2.1 5.0 collective-permute-start.1
  7.1 0.8 negate_select_fusion
  7.8 0.8 negate_select_fusion.1
  8.6 0.7 negate_select_fusion.3
  9.3 0.7 negate_select_fusion.6
  10.0 0.7 broadcast_compare_fusion
  10.7 0.7 broadcast_compare_fusion.1
  11.4 0.6 fusion.186
  12.1 0.7 fusion.187
  12.8 0.7 sign_compare_fusion
  13.5 0.7 sign_compare_fusion.1
  14.1 2.3 constant_dynamic-update-slice_fusion.1
  16.5 1.2 fusion.243
  17.8 1.1 constant_dynamic-update-slice_fusion
  19.5 0.8 broadcast_maximum_fusion.2
  20.4 0.7 multiply_reduce_fusion
  21.0 1.8 multiply_reduce_fusion.1
  22.9 106.7 %all-reduce = (f32[2,16,16]{2,1,0:T(8,128)S(1)}, f32[2,16,16]{2,1,0:T(8,128)S(1)}) all-reduce(f32[2,16,16]{2,1,0:T(8,128)S(1)} %multiply_reduce_fusion.1, f32[2,16,16]{2,1,0:T(8,128)S(1)} %multiply_reduce_fusion), channel_id=1, replica_groups=mesh['space'=8,'vel'=32] {'vel'}, use_global_device_ids=true, to_apply=%region_1.2 | all-reduce | flops 1024 | bytes 8192 | tf_op jit(solution)/shard_map/psum | solution.py:223
  129.8 1.4 copy-done.1
  131.2 0.6 copy-done.2
  131.8 0.9 select_select_fusion
  132.7 0.9 copy-done.6
  133.7 2.4 fusion.163
  136.1 0.9 convolution_bitcast_fusion.5
  137.0 35.0 %all-gather.6 = f32[32,4,256]{2,1,0:T(4,128)S(1)} all-gather(f32[1,4,256]{2,1,0:T(4,128)S(1)} %convolution_bitcast_fusion.5), channel_id=2, replica_groups=mesh['space'=8,'vel'=32] {'vel'}, dimensions={0}, use_global_device_ids=true | all-gather | bytes 135168 | tf_op jit(solution)/shard_map/all_gather | solution.py:19
  172.3 0.9 fusion.229
  173.6 52.5 %psum.68 = f32[4,256]{1,0:T(4,128)S(1)} all-reduce(f32[4,256]{1,0:T(4,128)S(1)} %pad_maximum_fusion.3), channel_id=1, replica_groups=mesh['space'=8,'vel'=32] {'vel'}, use_global_device_ids=true, to_apply=%region_9.10 | all-reduce | flops 1024 | bytes 8192 | tf_op jit(solution)/shard_map/psum | solution.py:172
  226.8 1.3 fusion.28
  228.0 0.9 convolution_bitcast_fusion.4
  228.9 33.2 %all-gather.7 = f32[32,4,256]{2,1,0:T(4,128)S(1)} all-gather(f32[1,4,256]{2,1,0:T(4,128)S(1)} %convolution_bitcast_fusion.4), channel_id=3, replica_groups=mesh['space'=8,'vel'=32] {'vel'}, dimensions={0}, use_global_device_ids=true | all-gather | bytes 135168 | tf_op jit(solution)/shard_map/all_gather | solution.py:19
  262.4 2.1 fusion.228
  264.9 52.7 %psum.69 = f32[4,256]{1,0:T(4,128)S(1)} all-reduce(f32[4,256]{1,0:T(4,128)S(1)} %pad_maximum_fusion.4), channel_id=1, replica_groups=mesh['space'=8,'vel'=32] {'vel'}, use_global_device_ids=true, to_apply=%region_15.16 | all-reduce | flops 1024 | bytes 8192 | tf_op jit(solution)/shard_map/psum | solution.py:172
  318.2 1.3 fusion.51
  319.5 0.9 convolution_bitcast_fusion.3
  320.4 33.2 %all-gather.8 = f32[32,4,256]{2,1,0:T(4,128)S(1)} all-gather(f32[1,4,256]{2,1,0:T(4,128)S(1)} %convolution_bitcast_fusion.3), channel_id=4, replica_groups=mesh['space'=8,'vel'=32] {'vel'}, dimensions={0}, use_global_device_ids=true | all-gather | bytes 135168 | tf_op jit(solution)/shard_map/all_gather | solution.py:19
  353.9 2.1 fusion.227
  356.4 52.5 %psum.70 = f32[4,256]{1,0:T(4,128)S(1)} all-reduce(f32[4,256]{1,0:T(4,128)S(1)} %pad_maximum_fusion.5), channel_id=1, replica_groups=mesh['space'=8,'vel'=32] {'vel'}, use_global_device_ids=true, to_apply=%region_21.22 | all-reduce | flops 1024 | bytes 8192 | tf_op jit(solution)/shard_map/psum | solution.py:172
  409.5 1.3 fusion.74
  410.8 1.2 fusion.239
  412.0 1.3 collective-permute-start.2
  413.3 5.0 collective-permute-start.3
  418.6 113.0 %psum.71 = f32[2,16,16]{2,1,0:T(8,128)S(1)} all-reduce(f32[2,16,16]{2,1,0:T(8,128)S(1)} %fusion.4), channel_id=1, replica_groups=mesh['space'=8,'vel'=32] {'vel'}, use_global_device_ids=true, to_apply=%region_23.24 | all-reduce | flops 512 | bytes 4096 | tf_op jit(solution)/shard_map/psum | solution.py:223
  531.9 1.3 copy-done.3
  533.3 0.9 fusion.5
  534.5 5.7 fusion.152
  540.2 0.9 convolution_bitcast_fusion.2
  541.1 35.0 %all-gather.9 = f32[32,4,256]{2,1,0:T(4,128)S(1)} all-gather(f32[1,4,256]{2,1,0:T(4,128)S(1)} %convolution_bitcast_fusion.2), channel_id=5, replica_groups=mesh['space'=8,'vel'=32] {'vel'}, dimensions={0}, use_global_device_ids=true | all-gather | bytes 135168 | tf_op jit(solution)/shard_map/all_gather | solution.py:19
  576.4 0.9 fusion.226
  577.7 52.5 %psum.72 = f32[4,256]{1,0:T(4,128)S(1)} all-reduce(f32[4,256]{1,0:T(4,128)S(1)} %pad_maximum_fusion.6), channel_id=1, replica_groups=mesh['space'=8,'vel'=32] {'vel'}, use_global_device_ids=true, to_apply=%region_29.30 | all-reduce | flops 1024 | bytes 8192 | tf_op jit(solution)/shard_map/psum | solution.py:172
  630.8 1.3 fusion.97
  632.1 0.9 convolution_bitcast_fusion.1
  633.0 33.4 %all-gather.10 = f32[32,4,256]{2,1,0:T(4,128)S(1)} all-gather(f32[1,4,256]{2,1,0:T(4,128)S(1)} %convolution_bitcast_fusion.1), channel_id=6, replica_groups=mesh['space'=8,'vel'=32] {'vel'}, dimensions={0}, use_global_device_ids=true | all-gather | bytes 135168 | tf_op jit(solution)/shard_map/all_gather | solution.py:19
  666.7 2.1 fusion.225
  669.2 52.5 %psum.73 = f32[4,256]{1,0:T(4,128)S(1)} all-reduce(f32[4,256]{1,0:T(4,128)S(1)} %pad_maximum_fusion.7), channel_id=1, replica_groups=mesh['space'=8,'vel'=32] {'vel'}, use_global_device_ids=true, to_apply=%region_35.36 | all-reduce | flops 1024 | bytes 8192 | tf_op jit(solution)/shard_map/psum | solution.py:172
  722.3 1.3 fusion.120
  723.6 0.9 convolution_bitcast_fusion
  724.5 33.2 %all-gather.11 = f32[32,4,256]{2,1,0:T(4,128)S(1)} all-gather(f32[1,4,256]{2,1,0:T(4,128)S(1)} %convolution_bitcast_fusion), channel_id=7, replica_groups=mesh['space'=8,'vel'=32] {'vel'}, dimensions={0}, use_global_device_ids=true | all-gather | bytes 135168 | tf_op jit(solution)/shard_map/all_gather | solution.py:19
  758.3 0.7 fusion.231
  759.2 2.1 fusion.224
  761.6 52.5 %psum.74 = f32[4,256]{1,0:T(4,128)S(1)} all-reduce(f32[4,256]{1,0:T(4,128)S(1)} %pad_maximum_fusion.8), channel_id=1, replica_groups=mesh['space'=8,'vel'=32] {'vel'}, use_global_device_ids=true, to_apply=%region_41.42 | all-reduce | flops 1024 | bytes 8192 | tf_op jit(solution)/shard_map/psum | solution.py:172
  814.2 0.7 slice_reduce_fusion.2
  814.9 0.7 slice.445
  816.2 2.0 fusion.143
  (214 shorter events, 10.1 us)
Async XLA Ops:
  0.6 15.8 %copy-start = (f32[1,16,16,1024]{3,2,1,0:T(8,128)S(1)}, f32[1,16,16,1024]{3,2,1,0:T(8,128)}, u32[]{:S(2)}) copy-start(f32[1,16,16,1024]{3,2,1,0:T(8,128)} %param.4) | copy-start | bytes 3145732
  0.6 132.1 %collective-permute-start = (f32[1,16,16,1024]{3,2,1,0:T(8,128)}, f32[1,16,16,1024]{3,2,1,0:T(8,128)S(1)}, u32[]{:S(2)}, u32[]{:S(2)}) collective-permute-start(f32[1,16,16,1024]{3,2,1,0:T(8,128)} %param.4), channel_id=1, source_target_pairs={{0,32},{32,64},{64,96},{96,128},{128,160},{160,192},{192,224},{1,3... | collective-permute-start | bytes 3145736 | tf_op jit(solution)/shard_map/ppermute | solution.py:31
  2.1 130.7 %collective-permute-start.1 = (f32[1,16,16,1024]{3,2,1,0:T(8,128)}, f32[1,16,16,1024]{3,2,1,0:T(8,128)}, u32[]{:S(2)}, u32[]{:S(2)}) collective-permute-start(f32[1,16,16,1024]{3,2,1,0:T(8,128)} %param.4), channel_id=1, source_target_pairs={{32,0},{64,32},{96,64},{128,96},{160,128},{192,160},{224,192},{33,... | collective-permute-start | bytes 3145736 | tf_op jit(solution)/shard_map/ppermute | solution.py:33
  16.5 1.3 copy-start.25
  17.7 1.3 copy-start.26
  20.3 113.4 %copy-start.7 = (f32[1024]{0:T(1024)}, f32[1024]{0:T(1024)S(1)}, u32[]{:S(2)}) copy-start(f32[1024]{0:T(1024)S(1)} %get-tuple-element.126) | copy-start | bytes 12292
  20.3 113.4 %copy-start.9 = (f32[1024]{0:T(1024)}, f32[1024]{0:T(1024)S(1)}, u32[]{:S(2)}) copy-start(f32[1024]{0:T(1024)S(1)} %get-tuple-element.180) | copy-start | bytes 12292
  20.3 109.5 %copy-start.21 = (f32[1024]{0:T(1024)}, f32[1024]{0:T(1024)S(1)}, u32[]{:S(2)}) copy-start(f32[1024]{0:T(1024)S(1)} %get-tuple-element.176) | copy-start | bytes 12292
  20.3 113.4 %copy-start.11 = (f32[1024]{0:T(1024)}, f32[1024]{0:T(1024)S(1)}, u32[]{:S(2)}) copy-start(f32[1024]{0:T(1024)S(1)} %get-tuple-element.175) | copy-start | bytes 12292
  20.3 113.4 %copy-start.13 = (f32[1024]{0:T(1024)}, f32[1024]{0:T(1024)S(1)}, u32[]{:S(2)}) copy-start(f32[1024]{0:T(1024)S(1)} %get-tuple-element.177) | copy-start | bytes 12292
  20.4 113.3 %copy-start.15 = (f32[1024]{0:T(1024)}, f32[1024]{0:T(1024)S(1)}, u32[]{:S(2)}) copy-start(f32[1024]{0:T(1024)S(1)} %get-tuple-element.178) | copy-start | bytes 12292
  22.9 107.0 %copy-start.17 = (pred[2,16,16]{2,1,0:T(8,128)(4,1)S(1)}, pred[2,16,16]{2,1,0:T(8,128)(4,1)}, u32[]{:S(2)}) copy-start(pred[2,16,16]{2,1,0:T(8,128)(4,1)} %get-tuple-element.128) | copy-start | bytes 1540
  22.9 107.0 %copy-start.19 = (pred[2,16,16]{2,1,0:T(8,128)(4,1)S(1)}, pred[2,16,16]{2,1,0:T(8,128)(4,1)}, u32[]{:S(2)}) copy-start(pred[2,16,16]{2,1,0:T(8,128)(4,1)} %get-tuple-element.129) | copy-start | bytes 1540
  129.6 189.9 %copy-start.23 = (f32[4]{0:T(128)}, f32[4]{0:T(128)S(1)}, u32[]{:S(2)}) copy-start(f32[4]{0:T(128)S(1)} %pad.34.clone) | copy-start | bytes 52
  129.6 1.6 copy-start.1
  129.6 2.2 copy-start.2
  131.8 1.9 copy-start.4
  132.7 1.0 copy-start.6
  412.0 122.2 %collective-permute-start.2 = (f32[1,16,16,1024]{3,2,1,0:T(8,128)S(1)}, f32[1,16,16,1024]{3,2,1,0:T(8,128)}, u32[]{:S(2)}, u32[]{:S(2)}) collective-permute-start(f32[1,16,16,1024]{3,2,1,0:T(8,128)S(1)} %fusion.74), channel_id=1, source_target_pairs={{0,32},{32,64},{64,96},{96,128},{128,160},{160,192},{192,224},{1,3... | collective-permute-start | bytes 3145736 | tf_op jit(solution)/shard_map/ppermute | solution.py:31
  413.3 120.9 %collective-permute-start.3 = (f32[1,16,16,1024]{3,2,1,0:T(8,128)S(1)}, f32[1,16,16,1024]{3,2,1,0:T(8,128)}, u32[]{:S(2)}, u32[]{:S(2)}) collective-permute-start(f32[1,16,16,1024]{3,2,1,0:T(8,128)S(1)} %fusion.74), channel_id=1, source_target_pairs={{32,0},{64,32},{96,64},{128,96},{160,128},{192,160},{224,192},{33,... | collective-permute-start | bytes 3145736 | tf_op jit(solution)/shard_map/ppermute | solution.py:33
  531.6 1.6 copy-start.3
  531.6 1.6 copy-start.18
  531.6 1.6 copy-start.20
  531.6 1.6 copy-start.22
  533.2 1.2 copy-start.5
  533.2 1.2 copy-start.8
  533.2 1.2 copy-start.10
  533.3 1.2 copy-start.12
  533.3 1.2 copy-start.14
  533.3 1.2 copy-start.16
  534.5 5.7 copy-start.24
